TPU v7x, 256 devices: a whole 4x4x8 slice. The times are simulated.
256 devices in a mesh: rep: 128 (over x_hi, z, y, core), grp: 2 (over x_lo).
Axes of the slice: x: 4 (x_hi: 2, x_lo: 2; x = x_hi * 2 + x_lo), y: 4, z: 8, core: 2. Of those that a mesh axis runs over, the one named last changes fastest.
Arguments:
- local_params: bfloat16 [128, 2, 256, 8192], P('rep', 'grp'), may hold values from -130 to 130
- snapshot: bfloat16 [2, 256, 8192], P('grp'), may hold values from -4 to 4
- master: float32 [2, 256, 8192], P('grp', 'rep'), may hold values from -6 to 6
- momentum: float32 [2, 256, 8192], P('grp', 'rep'), may hold values from -4 to 4
Outputs:
- new_master: float32 [2, 256, 8192], P('grp', 'rep')
- new_momentum: float32 [2, 256, 8192], P('grp', 'rep')
- new_params: bfloat16 [2, 256, 8192], P('grp')
All inputs are finite; a program needn't handle non-finite values.
Results may differ from a plain program's by a relative error of at most 0.001.
Values may be sent and summed in bfloat16 or wider, within the bound.
No kernel may reach another device: no remote copies, remote signals or barrier semaphores. Data moves between devices by JAX's collectives and lax.ppermute only.
A program may use at most 128 MiB of HBM per device.

v0:
```python
import functools

import jax
import jax.numpy as jnp
from jax import lax
from jax.sharding import Mesh
from jax.sharding import PartitionSpec as P

REP = ("rep_0", "rep_1", "rep_2", "rep_3")
REP_GRP = ("rep_0", "rep_1", "rep_2", "rep_3", "grp")


nesterov_mu = 0.9
outer_rate = 0.7
clip_limit = 0.15
epsilon = 1e-06


def split_up(x, dim, size):
    lengths = x.shape
    parts = x.reshape(*lengths[:dim], size, lengths[dim] // size, *lengths[dim + 1 :])
    return jnp.moveaxis(parts, dim, 0)


def sum_at_owner(x, axis, dim):
    parts = split_up(x, dim, lax.axis_size(axis))
    arrived = lax.all_to_all(parts, axis, split_axis=0, concat_axis=0, tiled=True)
    return arrived.sum(axis=0)


def sum_in_two_steps(x, axes, dim):
    far, near = axes
    own = sum_at_owner(split_up(x, dim, lax.axis_size(far)), near, dim + 1)
    return jnp.sum(lax.all_to_all(own, far, 0, 0, tiled=True), axis=0)


def one_axis_at_a_time(x, axes):
    return functools.reduce(lax.psum, axes, x)


def copy_for_each(x, axis):
    size = lax.axis_size(axis)
    return lax.all_to_all(jnp.broadcast_to(x[None], (size, *x.shape)), axis, 0, 0, tiled=True)


def laid_out(parts, dim):
    lengths = list(parts.shape[1:])
    lengths[dim] *= parts.shape[0]
    return jnp.moveaxis(parts, 0, dim).reshape(lengths)


def whole_of(x, axes, dim):
    far, near = axes
    first = copy_for_each(x, far)
    parts = jnp.swapaxes(copy_for_each(first, near), 0, 1)
    return laid_out(parts.reshape(-1, *x.shape), dim)


def body(local_params, snapshot, master, momentum):
    replicas = lax.axis_size(REP)
    snapshot_rows = snapshot[0]
    local_rows = local_params[0, 0]
    start_rows = snapshot_rows.astype(jnp.float32)
    end_rows = local_rows.astype(jnp.float32)
    summed = sum_in_two_steps(start_rows - end_rows, (("rep_0", "rep_1", "rep_2"), "rep_3"), 0)
    outer_grad = (summed / replicas)[None]
    elements = snapshot.shape[1] * snapshot.shape[2] * lax.axis_size("grp")
    squares = one_axis_at_a_time(jnp.sum(outer_grad * outer_grad), REP_GRP)
    grad_rms = jnp.sqrt(squares / elements + epsilon)
    clipped = jnp.minimum(1.0, clip_limit / grad_rms) * outer_grad
    new_momentum = nesterov_mu * momentum + clipped
    new_master = master - outer_rate * (clipped + nesterov_mu * new_momentum)
    new_params = whole_of(
        new_master.astype(jnp.bfloat16), (("rep_0", "rep_1", "rep_2"), "rep_3"), 1
    )
    return (new_master, new_momentum, new_params)


def solution(mesh):
    finer = Mesh(
        mesh.devices.reshape(2, 8, 4, 2, mesh.shape["grp"]),
        ("rep_0", "rep_1", "rep_2", "rep_3", "grp"),
    )
    in_specs = (
        P(REP, "grp", None, None),
        P("grp", None, None),
        P("grp", REP, None),
        P("grp", REP, None),
    )
    out_specs = (P("grp", REP, None), P("grp", REP, None), P("grp", None, None))
    return jax.shard_map(body, mesh=finer, in_specs=in_specs, out_specs=out_specs, check_vma=False)
```

profile of v0, /device:TPU:1, one launch (start us, length us, event | category | flops | bytes accessed | tf_op | source)
XLA Modules:
  0.0 301.1 jit_solution(1633917752148891616)
XLA Ops:
  0.6 9.7 %reshape.31 = f32[64,2,2,8192]{3,2,1,0:T(2,128)} reshape(bf16[1,1,256,8192]{3,2,1,0:T(8,128)(2,1)} %param.4) | data formatting | bytes 12582912 | tf_op jit(solution)/shard_map/convert_element_type | solution.py:64
  10.4 9.7 %reshape.30 = f32[64,2,2,8192]{3,2,1,0:T(2,128)} reshape(bf16[1,256,8192]{2,1,0:T(8,128)(2,1)} %param.5) | data formatting | bytes 12582912 | tf_op jit(solution)/shard_map/convert_element_type | solution.py:63
  20.0 7.2 %subtract_bitcast_fusion = f32[2,64,2,8192]{3,2,0,1:T(2,128)S(1)} fusion(f32[64,2,2,8192]{3,2,1,0:T(2,128)} %reshape.30, f32[64,2,2,8192]{3,2,1,0:T(2,128)} %reshape.31), kind=kLoop, calls=%fused_computation | loop fusion | flops 2097152 | bytes 25165824 | tf_op jit(solution)/shard_map/transpose | solution.py:22
  27.3 1.7 copy.11
  29.0 14.6 %all_to_all.20 = f32[2,64,2,8192]{3,2,1,0:T(2,128)} all-to-all(f32[2,64,2,8192]{3,2,1,0:T(2,128)S(1)} %copy.11), channel_id=1, replica_groups=mesh['rep_0'=2,'rep_1'=8,'rep_2'=4,'rep_3'=2,'grp'=2] {'rep_3'}, dimensions={0} | all-to-all | bytes 16777216 | tf_op jit(solution)/shard_map/all_to_all | solution.py:27
  43.6 12.0 %reduce_sum.27 = f32[64,2,8192]{2,1,0:T(2,128)} reduce(f32[2,64,2,8192]{3,2,1,0:T(2,128)} %all_to_all.20, f32[]{:T(128)} %constant.2.clone.1), dimensions={0}, to_apply=%region_0.0 | reduce | flops 1048576 | bytes 12582916 | tf_op jit(solution)/shard_map/reduce_sum | solution.py:28
  55.6 107.2 %all_to_all.21 = f32[64,2,8192]{2,1,0:T(2,128)} all-to-all(f32[64,2,8192]{2,1,0:T(2,128)} %reduce_sum.27), channel_id=1, replica_groups=mesh['rep_0'=2,'rep_1'=8,'rep_2'=4,'rep_3'=2,'grp'=2] {'rep_0','rep_1','..., dimensions={0} | all-to-all | bytes 8388608 | tf_op jit(solution)/shard_map/all_to_all | solution.py:34
  162.8 0.0 copy-start
  162.8 0.0 copy-start.1
  162.8 3.6 %reduce_sum.28 = f32[2,8192]{1,0:T(2,128)S(1)} reduce(f32[64,2,8192]{2,1,0:T(2,128)} %all_to_all.21, f32[]{:T(128)} %constant.2.clone.1), dimensions={0}, to_apply=%region_1.0 | reduce | flops 1032192 | bytes 4259844 | tf_op jit(solution)/shard_map/reduce_sum | solution.py:34
  166.4 0.7 multiply_reduce_fusion
  167.1 5.9 %psum.35 = f32[]{:T(128)} all-reduce(f32[]{:T(128)} %multiply_reduce_fusion), channel_id=1, replica_groups=mesh['rep_0'=2,'rep_1'=8,'rep_2'=4,'rep_3'=2,'grp'=2] {'rep_0'}, use_global_device_ids=true, to_apply=%region_3.0 | all-reduce | flops 1 | bytes 8 | tf_op jit(solution)/shard_map/psum | solution.py:38
  172.9 14.5 %psum.36 = f32[]{:T(128)} all-reduce(f32[]{:T(128)} %psum.35), channel_id=1, replica_groups=mesh['rep_0'=2,'rep_1'=8,'rep_2'=4,'rep_3'=2,'grp'=2] {'rep_1'}, use_global_device_ids=true, to_apply=%region_4.0 | all-reduce | flops 1 | bytes 8 | tf_op jit(solution)/shard_map/psum | solution.py:38
  187.4 8.6 %psum.37 = f32[]{:T(128)} all-reduce(f32[]{:T(128)} %psum.36), channel_id=1, replica_groups=mesh['rep_0'=2,'rep_1'=8,'rep_2'=4,'rep_3'=2,'grp'=2] {'rep_2'}, use_global_device_ids=true, to_apply=%region_5.0 | all-reduce | flops 1 | bytes 8 | tf_op jit(solution)/shard_map/psum | solution.py:38
  196.0 11.5 %psum.38 = f32[]{:T(128)} all-reduce(f32[]{:T(128)} %psum.37), channel_id=1, replica_groups=mesh['rep_0'=2,'rep_1'=8,'rep_2'=4,'rep_3'=2,'grp'=2] {'rep_3'}, use_global_device_ids=true, to_apply=%region_6.0 | all-reduce | flops 1 | bytes 8 | tf_op jit(solution)/shard_map/psum | solution.py:38
  207.6 4.4 %psum.39 = f32[]{:T(128)} all-reduce(f32[]{:T(128)} %psum.38), channel_id=1, replica_groups=mesh['rep_0'=2,'rep_1'=8,'rep_2'=4,'rep_3'=2,'grp'=2] {'grp'}, use_global_device_ids=true, to_apply=%region_7.0 | all-reduce | flops 1 | bytes 8 | tf_op jit(solution)/shard_map/psum | solution.py:38
  212.7 0.0 copy-done
  212.7 0.0 copy-done.1
  212.7 0.8 convert_bitcast_fusion
  213.5 2.0 broadcast_in_dim.18
  215.5 53.8 %all_to_all.22 = bf16[64,1,2,8192]{3,2,1,0:T(2,128)(2,1)S(1)} all-to-all(bf16[64,1,2,8192]{3,2,1,0:T(2,128)(2,1)S(1)} %broadcast_in_dim.18), channel_id=1, replica_groups=mesh['rep_0'=2,'rep_1'=8,'rep_2'=4,'rep_3'=2,'grp'=2] {'rep_0','rep_1','..., dimensions={0} | all-to-all | bytes 4194304 | tf_op jit(solution)/shard_map/all_to_all | solution.py:43
  269.3 6.2 %broadcast_in_dim.20 = bf16[2,64,1,2,8192]{4,3,1,2,0:T(2,128)(2,1)} broadcast(bf16[64,2,8192]{2,1,0:T(2,128)(2,1)S(1)} %bitcast.20), dimensions={1,3,4} | broadcast | bytes 6291456 | tf_op jit(solution)/shard_map/broadcast_in_dim | solution.py:43
  275.5 12.5 %all_to_all.23 = bf16[2,64,1,2,8192]{4,3,1,2,0:T(2,128)(2,1)S(1)} all-to-all(bf16[2,64,1,2,8192]{4,3,1,2,0:T(2,128)(2,1)} %broadcast_in_dim.20), channel_id=1, replica_groups=mesh['rep_0'=2,'rep_1'=8,'rep_2'=4,'rep_3'=2,'grp'=2] {'rep_3'}, dimensions={0} | all-to-all | bytes 8388608 | tf_op jit(solution)/shard_map/all_to_all | solution.py:43
  288.0 5.9 %copy.13 = bf16[64,2,1,2,8192]{4,3,1,0,2:T(2,128)(2,1)} copy(bf16[64,2,1,2,8192]{4,3,0,2,1:T(2,128)(2,1)S(1)} %bitcast.19) | data formatting | bytes 8388608 | tf_op jit(solution)/shard_map/transpose | solution.py:55
  293.9 7.2 %reshape_transpose_reshape.3 = bf16[1,256,8192]{2,1,0:T(8,128)(2,1)} reshape(bf16[64,2,1,2,8192]{4,3,1,0,2:T(2,128)(2,1)} %copy.13) | data formatting | bytes 8388608 | tf_op jit(solution)/shard_map/reshape;transpose;reshape | solution.py:49
Async XLA Ops:
  162.8 49.9 %copy-start = (f32[1,2,8192]{2,1,0:T(2,128)S(1)}, f32[1,2,8192]{2,1,0:T(2,128)}, u32[]{:S(2)}) copy-start(f32[1,2,8192]{2,1,0:T(2,128)} %param.6) | copy-start | bytes 196612
  162.8 49.9 %copy-start.1 = (f32[1,2,8192]{2,1,0:T(2,128)S(1)}, f32[1,2,8192]{2,1,0:T(2,128)}, u32[]{:S(2)}) copy-start(f32[1,2,8192]{2,1,0:T(2,128)} %param.7) | copy-start | bytes 196612
where the time goes:
time: 302 us; the launch traced here: 301 us
  blocking collectives  233 us (77%)
  local copies, waits for them, and re-layouts  42.4 us (14%)
  other arithmetic  24.3 us (8%)
    all_to_all x1, blocking collectives, sum_in_two_steps(): return jnp.sum(lax.all_to_all(own, far, 0, 0, tiled=True), axis=0)  107 us
    all_to_all x2, blocking collectives, copy_for_each(): lax.all_to_all(jnp.broadcast_to(x[None], (size, *x.shape)), axis, 0, 0, t...  66.3 us
    psum x5, blocking collectives, one_axis_at_a_time(): return functools.reduce(lax.psum, axes, x)  44.9 us
    all_to_all x1, blocking collectives, sum_at_owner(): lax.all_to_all(parts, axis, split_axis=0, concat_axis=0, tiled=True)  14.6 us
    reduce_sum x1, other arithmetic, sum_at_owner(): return arrived.sum(axis=0)  12 us
    convert_element_type x1, local copies, waits for them, and re-layouts, body(): end_rows = local_rows.astype(jnp.float32)  9.72 us
    convert_element_type x1, local copies, waits for them, and re-layouts, body(): start_rows = snapshot_rows.astype(jnp.float32)  9.67 us
    broadcast_in_dim x2, local copies, waits for them, and re-layouts, copy_for_each(): jnp.broadcast_to(x[None], (size, *x.shape))  8.24 us

commit v1 on v0

v1 whole, which is shorter than its diff:
```python
import functools

import jax
import jax.numpy as jnp
from jax import lax
from jax.experimental import pallas as pl
from jax.experimental.pallas import tpu as pltpu
from jax.sharding import Mesh
from jax.sharding import PartitionSpec as P

REP = ("xh", "z", "y", "c")
ALL = ("xh", "z", "y", "c", "g")

nesterov_mu = 0.9
outer_rate = 0.7
clip_limit = 0.15
epsilon = 1e-06

SCALE = 32.0


def shift(axis, by):
    n = lax.axis_size(axis)
    return [(i, (i + by) % n) for i in range(n)]


def to_blocks_kernel(at, own, other, start, *outs):
    n = len(outs)
    rows, cols = own.shape
    per = rows // n
    mine = at[1]
    o = lax.broadcasted_iota(jnp.int32, (rows, rows), 0)
    r = lax.broadcasted_iota(jnp.int32, (rows, rows), 1)
    b, q = (o % per) // 4, o % 4
    dest = (o // per + mine) % n
    hit = r == b * (4 * n) + dest * 4 + q
    one = jnp.where(hit, -SCALE, 0.0).astype(jnp.bfloat16)
    two = jnp.where(hit, 2 * SCALE, 0.0).astype(jnp.bfloat16)
    dot = functools.partial(jnp.dot, preferred_element_type=jnp.float32)
    s = dot(two, start[...]) + (dot(one, own[...]) + dot(one, other[...]))
    for j, out in enumerate(outs):
        out[...] = s[j * per : (j + 1) * per].astype(out.dtype)


def to_blocks(at, own, other, start, n, wire, width=512):
    rows, half = other.shape
    steps = half // width
    mine = pl.BlockSpec((rows, width), lambda k, at: (0, at[0] * steps + k))
    plain = pl.BlockSpec((rows, width), lambda k, at: (0, k))
    return pl.pallas_call(
        to_blocks_kernel,
        grid_spec=pltpu.PrefetchScalarGridSpec(
            num_scalar_prefetch=1,
            grid=(steps,),
            in_specs=[mine, plain, mine],
            out_specs=[pl.BlockSpec((rows // n, width), lambda k, at: (0, k))] * n,
        ),
        out_shape=[jax.ShapeDtypeStruct((rows // n, half), wire)] * n,
        name="to_blocks",
    )(at, own, other, start)


def from_blocks_kernel(at, *refs):
    *ins, out = refs
    n = len(ins) // 2
    per = ins[0].shape[0]
    rows = n * per
    mine = at[1]
    r = lax.broadcasted_iota(jnp.int32, (rows, rows), 0)
    o = lax.broadcasted_iota(jnp.int32, (rows, rows), 1)
    b, q = (o % per) // 4, o % 4
    src = (mine - o // per + n) % n
    one = jnp.where(r == b * (4 * n) + src * 4 + q, 1.0, 0.0).astype(jnp.bfloat16)

    def place(blocks):
        x = jnp.concatenate([ref[...] for ref in blocks], axis=0)
        out[...] = jnp.dot(one, x, preferred_element_type=jnp.float32).astype(out.dtype)

    @pl.when(pl.program_id(0) == 0)
    def _():
        place(ins[:n])

    @pl.when(pl.program_id(0) == 1)
    def _():
        place(ins[n:])


def from_blocks(at, mine, others, width=512):
    n = len(mine)
    per, half = mine[0].shape
    steps = half // width
    first = pl.BlockSpec((per, width), lambda h, k, at: (0, jnp.where(h == 0, k, steps - 1)))
    second = pl.BlockSpec((per, width), lambda h, k, at: (0, jnp.where(h == 0, 0, k)))
    out = pl.BlockSpec((n * per, width), lambda h, k, at: (0, ((at[0] + h) % 2) * steps + k))
    return pl.pallas_call(
        from_blocks_kernel,
        grid_spec=pltpu.PrefetchScalarGridSpec(
            num_scalar_prefetch=1,
            grid=(2, steps),
            in_specs=[first] * n + [second] * n,
            out_specs=out,
        ),
        out_shape=jax.ShapeDtypeStruct((n * per, 2 * half), mine[0].dtype),
        name="from_blocks",
    )(at, *mine, *others)


def body(local_params, snapshot, master, momentum):
    replicas = lax.axis_size(REP)
    core, ys = lax.axis_index("c"), lax.axis_size("y")
    at = jnp.stack([core, lax.axis_index("y")]).astype(jnp.int32)
    local, start = local_params[0, 0], snapshot[0]
    rows, cols = local.shape
    half = cols // 2
    swap = shift("c", 1)

    send = lax.dynamic_slice(local, (0, (1 - core) * half), (rows, half))
    other = lax.ppermute(send, "c", swap)
    blocks = to_blocks(at, local, other, start, ys, jnp.float32)
    arrived = [lax.ppermute(blocks[j].astype(jnp.float16), "y", shift("y", j)) for j in (2, 1, 3)]
    total = blocks[0]
    for x in arrived:
        total = total + x.astype(jnp.float32)
    near = total.astype(jnp.float16).reshape(-1, 2, half)
    own = lax.all_to_all(near, ("xh", "z", "c"), 0, 0, tiled=True)
    summed = own.reshape(-1, 2, 2, half).astype(jnp.float32).sum(axis=0)
    outer_grad = jnp.swapaxes(summed, 0, 1).reshape(1, 2, cols) * (1.0 / (SCALE * replicas))

    part = jnp.sum(outer_grad * outer_grad)
    members = lax.axis_size(ALL)
    parts = lax.all_to_all(jnp.full((members, 1, 128), part), ALL, 0, 0, tiled=True)
    squares = jnp.sum(parts[:, 0, 0])
    elements = rows * cols * lax.axis_size("g")
    grad_rms = jnp.sqrt(squares / elements + epsilon)
    clipped = jnp.minimum(1.0, clip_limit / grad_rms) * outer_grad
    new_momentum = nesterov_mu * momentum + clipped
    new_master = master - outer_rate * (clipped + nesterov_mu * new_momentum)

    new_rows = jnp.swapaxes(new_master[0].astype(jnp.bfloat16).reshape(2, 2, half), 0, 1)
    sent = jnp.broadcast_to(new_rows[None], (near.shape[0] // 2, 2, 2, half)).reshape(near.shape)
    mine = lax.all_to_all(sent, ("xh", "z", "c"), 0, 0, tiled=True).reshape(-1, half)
    got = {j: lax.ppermute(mine, "y", shift("y", j)) for j in (2, 1, 3)}
    got[0] = mine
    got = [got[j] for j in range(ys)]
    theirs = [lax.ppermute(x, "c", swap) for x in got]
    new_params = from_blocks(at, got, theirs)
    return (new_master, new_momentum, new_params[None])


def solution(mesh):
    finer = Mesh(mesh.devices.reshape(2, 8, 4, 2, mesh.shape["grp"]), ALL)
    in_specs = (
        P(REP, "g", None, None),
        P("g", None, None),
        P("g", REP, None),
        P("g", REP, None),
    )
    out_specs = (P("g", REP, None), P("g", REP, None), P("g", None, None))
    return jax.shard_map(body, mesh=finer, in_specs=in_specs, out_specs=out_specs, check_vma=False)
```

time: 302 us -> 170 us (0.56)
  blocking collectives: 233 us -> 73.3 us
  waiting for transfers between devices: 0 us -> 41.3 us
  local copies, waits for them, and re-layouts: 42.4 us -> 4.42 us
  Pallas kernels: 0 us -> 21.4 us
  starting transfers between devices: 0 us -> 19.1 us
  other arithmetic: 24.3 us -> 7.59 us
    all_to_all x4 -> x3, blocking collectives: 188 us -> 73.3 us  [the longest x1 31.5 us: body(): own = lax.all_to_all(near, ('xh', 'z', 'c'), 0, 0, tiled=True)]
    psum x5 -> x0, blocking collectives: 44.9 us -> none  [one_axis_at_a_time(): return functools.reduce(lax.psum, axes, x)]
    ppermute x0 -> x11, waiting for transfers between devices: none -> 41.3 us  [the longest x3 22.6 us: body(): lax.ppermute(blocks[j].astype(jnp.float16), 'y', shift('y', j))]
    pallas_call x0 -> x2, Pallas kernels: none -> 21.4 us  [the longest x1 12.8 us: from_blocks(): pl.pallas_call(from_blocks_kernel, grid_spec=pltpu.PrefetchScalarGridSpec...]
    convert_element_type x2 -> x1, local copies, waits for them, and re-layouts: 19.4 us -> 0.03 us  [body(): new_master[0].astype(jnp.bfloat16).reshape(2, 2, half)]
    ppermute x0 -> x11, starting transfers between devices: none -> 19.1 us  [the longest x4 10.9 us: body(): theirs = [lax.ppermute(x, 'c', swap) for x in got]]
    reduce_sum x3, other arithmetic: 16.3 us -> 1.99 us  [the longest x1 0.87 us: body(): squares = jnp.sum(parts[:, 0, 0])]
    transpose x2 -> x1, local copies, waits for them, and re-layouts: 7.64 us -> 0.04 us  [body(): jnp.swapaxes(new_master[0].astype(jnp.bfloat16).reshape(2, 2, half), 0, 1)]
  transfers between devices with their start and end apart: 0 -> 11, of which waited for: 0 -> 7; matrix products, arithmetic and copies ran while one was open for 0% -> 0% of each run, Pallas kernels for 0% -> 0%
where the time goes in v1:
time: 170 us; the launch traced here: 169 us
  blocking collectives  73.3 us (43%)
  waiting for transfers between devices  41.3 us (24%)
  Pallas kernels  21.4 us (13%)
  starting transfers between devices  19.1 us (11%)
  other arithmetic  7.59 us (4%)
  local copies, waits for them, and re-layouts  4.42 us (3%)
    all_to_all x1, blocking collectives, body(): own = lax.all_to_all(near, ('xh', 'z', 'c'), 0, 0, tiled=True)  31.5 us
    ppermute x3, waiting for transfers between devices, body(): lax.ppermute(blocks[j].astype(jnp.float16), 'y', shift('y', j))  22.6 us
    all_to_all x1, blocking collectives, body(): lax.all_to_all(sent, ('xh', 'z', 'c'), 0, 0, tiled=True).reshape(-1, half)  22 us
    all_to_all x1, blocking collectives, body(): lax.all_to_all(jnp.full((members, 1, 128), part), ALL, 0, 0, tiled=True)  19.8 us
    ppermute x3, waiting for transfers between devices, body(): got = {j: lax.ppermute(mine, 'y', shift('y', j)) for j in (2, 1, 3)}  14.6 us
    pallas_call x1, Pallas kernels, from_blocks(): pl.pallas_call(from_blocks_kernel, grid_spec=pltpu.PrefetchScalarGridSpec...  12.8 us
    ppermute x4, starting transfers between devices, body(): theirs = [lax.ppermute(x, 'c', swap) for x in got]  10.9 us
    pallas_call x1, Pallas kernels, to_blocks(): pl.pallas_call(to_blocks_kernel, grid_spec=pltpu.PrefetchScalarGridSpec(n...  8.65 us
  transfers between devices with their start and end apart: 11, of which 7 were waited for; matrix products, arithmetic and copies ran while one was open for 0% of the time, Pallas kernels for 0%

profile of v1, /device:TPU:1, one launch (start us, length us, event | category | flops | bytes accessed | tf_op | source)
XLA Modules:
  0.0 168.6 jit_solution(4172817740233146610)
XLA Ops:
  0.6 1.7 %dynamic-slice_bitcast_fusion = bf16[256,4096]{1,0:T(8,128)(2,1)S(1)} fusion(bf16[1,1,256,8192]{3,2,1,0:T(8,128)(2,1)} %param.4, s32[]{:T(128)S(6)} %select_n.3), kind=kLoop, calls=%fused_computation | loop fusion | bytes 4194308 | tf_op jit(solution)/shard_map/dynamic_slice | solution.py:117
  2.4 3.3 %collective-permute-start = (bf16[256,4096]{1,0:T(8,128)(2,1)S(1)}, bf16[256,4096]{1,0:T(8,128)(2,1)}, u32[]{:S(2)}, u32[]{:S(2)}) collective-permute-start(bf16[256,4096]{1,0:T(8,128)(2,1)S(1)} %dynamic-slice_bitcast_fusion), channel_id=1, source_target_pairs={{0,2},{2,0},{1,3},{3,1},{4,6},{6,4},{5,7},{7,5},{8,10},{10,8},{9,1... | collective-permute-start | bytes 6291464 | tf_op jit(solution)/shard_map/ppermute | solution.py:118
  5.7 0.6 pad_add_fusion.at
  6.3 3.3 %collective-permute-done.other = bf16[256,4096]{1,0:T(8,128)(2,1)} collective-permute-done((bf16[256,4096]{1,0:T(8,128)(2,1)S(1)}, bf16[256,4096]{1,0:T(8,128)(2,1)}, u32[]{:S(2)}, u32[]{:S(2)}) %collective-permute-start) | collective-permute-done | bytes 2097184 | tf_op jit(solution)/shard_map/ppermute | solution.py:118
  9.6 8.7 %to_blocks.1 = (f32[64,4096]{1,0:T(8,128)}, f32[64,4096]{1,0:T(8,128)}, f32[64,4096]{1,0:T(8,128)}, f32[64,4096]{1,0:T(8,128)}) custom-call(s32[2]{0:T(128)} %pad_add_fusion.at, bf16[256,8192]{1,0:T(8,128)(2,1)} %bitcast.14, bf16[256,4096]{1,0:T(8,128)(2,1)} %collective-permute-done.other, bf16[256,8192]{1,0:T(8,128)(2,1)} %bitcast.15), custom_call_target="tpu_custom_call" | custom-call | tf_op jit(solution)/shard_map/to_blocks/pallas_call | solution.py:50
  18.2 1.4 convert_element_type.34
  19.6 1.3 convert_element_type.36
  20.9 0.0 copy-start.8
  20.9 0.0 copy-start.9
  20.9 1.3 convert_element_type.38
  22.2 1.1 collective-permute-start.3
  23.3 0.4 collective-permute-start.2
  23.8 1.2 collective-permute-start.1
  25.0 10.4 %collective-permute-done.3 = f16[64,4096]{1,0:T(8,128)(2,1)S(1)} collective-permute-done((f16[64,4096]{1,0:T(8,128)(2,1)S(1)}, f16[64,4096]{1,0:T(8,128)(2,1)S(1)}, u32[]{:S(2)}, u32[]{:S(2)}) %collective-permute-start.3) | collective-permute-done | bytes 524320 | tf_op jit(solution)/shard_map/ppermute | solution.py:120
  35.4 3.0 %collective-permute-done.2 = f16[64,4096]{1,0:T(8,128)(2,1)S(1)} collective-permute-done((f16[64,4096]{1,0:T(8,128)(2,1)S(1)}, f16[64,4096]{1,0:T(8,128)(2,1)S(1)}, u32[]{:S(2)}, u32[]{:S(2)}) %collective-permute-start.2) | collective-permute-done | bytes 524320 | tf_op jit(solution)/shard_map/ppermute | solution.py:120
  38.4 9.2 %collective-permute-done.1 = f16[64,4096]{1,0:T(8,128)(2,1)S(1)} collective-permute-done((f16[64,4096]{1,0:T(8,128)(2,1)S(1)}, f16[64,4096]{1,0:T(8,128)(2,1)S(1)}, u32[]{:S(2)}, u32[]{:S(2)}) %collective-permute-start.1) | collective-permute-done | bytes 524320 | tf_op jit(solution)/shard_map/ppermute | solution.py:120
  47.6 0.3 add_convert_fusion
  47.9 0.4 reshape.42
  48.3 31.5 %all_to_all.15 = f16[32,2,4096]{2,1,0:T(2,128)(2,1)S(1)} all-to-all(f16[32,2,4096]{2,1,0:T(2,128)(2,1)S(1)} %reshape.42), channel_id=1, replica_groups=mesh['xh'=2,'z'=8,'y'=4,'c'=2,'g'=2] {'xh','z','c'}, dimensions={0} | all-to-all | bytes 1048576 | tf_op jit(solution)/shard_map/all_to_all | solution.py:125
  79.7 0.4 convert_reduce_fusion
  80.2 0.7 multiply_reduce_fusion
  80.8 0.7 broadcast_in_dim.12
  81.6 19.8 %all_to_all.16 = f32[256,1,128]{2,1,0:T(1,128)S(1)} all-to-all(f32[256,1,128]{2,1,0:T(1,128)S(1)} %broadcast_in_dim.12), channel_id=1, replica_groups=mesh['xh'=2,'z'=8,'y'=4,'c'=2,'g'=2] {'xh','z','y','c','g'}, dimensions={0} | all-to-all | bytes 262144 | tf_op jit(solution)/shard_map/all_to_all | solution.py:131
  101.4 0.9 slice_reduce_fusion
  103.0 0.0 copy-done.8
  103.0 0.0 copy-done.9
  103.0 0.8 fusion
  103.8 0.5 broadcast_in_dim.13
  104.3 22.0 %all_to_all.17 = bf16[32,2,4096]{2,1,0:T(2,128)(2,1)S(1)} all-to-all(bf16[32,2,4096]{2,1,0:T(2,128)(2,1)S(1)} %bitcast.18), channel_id=1, replica_groups=mesh['xh'=2,'z'=8,'y'=4,'c'=2,'g'=2] {'xh','z','c'}, dimensions={0} | all-to-all | bytes 1048576 | tf_op jit(solution)/shard_map/all_to_all | solution.py:141
  126.3 0.2 reshape.44.refs_0_
  126.5 0.0 copy-start
  126.5 0.6 collective-permute-start.6
  127.1 1.6 collective-permute-start.5
  128.7 0.0 collective-permute-start.4
  128.7 2.6 %collective-permute-start.7 = (bf16[64,4096]{1,0:T(8,128)(2,1)S(1)}, bf16[64,4096]{1,0:T(8,128)(2,1)S(1)}, u32[]{:S(2)}, u32[]{:S(2)}) collective-permute-start(bf16[64,4096]{1,0:T(8,128)(2,1)S(1)} %reshape.44.refs_0_), channel_id=1, source_target_pairs={{0,2},{2,0},{1,3},{3,1},{4,6},{6,4},{5,7},{7,5},{8,10},{10,8},{9,1... | collective-permute-start | bytes 1572872 | tf_op jit(solution)/shard_map/ppermute | solution.py:145
  131.3 6.7 %collective-permute-done.6.refs_3_ = bf16[64,4096]{1,0:T(8,128)(2,1)S(1)} collective-permute-done((bf16[64,4096]{1,0:T(8,128)(2,1)S(1)}, bf16[64,4096]{1,0:T(8,128)(2,1)S(1)}, u32[]{:S(2)}, u32[]{:S(2)}) %collective-permute-start.6) | collective-permute-done | bytes 524320 | tf_op jit(solution)/shard_map/ppermute | solution.py:142
  138.0 5.4 %collective-permute-start.10 = (bf16[64,4096]{1,0:T(8,128)(2,1)S(1)}, bf16[64,4096]{1,0:T(8,128)(2,1)S(1)}, u32[]{:S(2)}, u32[]{:S(2)}) collective-permute-start(bf16[64,4096]{1,0:T(8,128)(2,1)S(1)} %collective-permute-done.6.refs_3_), channel_id=1, source_target_pairs={{0,2},{2,0},{1,3},{3,1},{4,6},{6,4},{5,7},{7,5},{8,10},{10,8},{9,1... | collective-permute-start | bytes 1572872 | tf_op jit(solution)/shard_map/ppermute | solution.py:145
  143.4 0.0 collective-permute-done.5.refs_2_
  143.4 2.3 %collective-permute-start.9 = (bf16[64,4096]{1,0:T(8,128)(2,1)S(1)}, bf16[64,4096]{1,0:T(8,128)(2,1)S(1)}, u32[]{:S(2)}, u32[]{:S(2)}) collective-permute-start(bf16[64,4096]{1,0:T(8,128)(2,1)S(1)} %collective-permute-done.5.refs_2_), channel_id=1, source_target_pairs={{0,2},{2,0},{1,3},{3,1},{4,6},{6,4},{5,7},{7,5},{8,10},{10,8},{9,1... | collective-permute-start | bytes 1572872 | tf_op jit(solution)/shard_map/ppermute | solution.py:145
  145.7 7.9 %collective-permute-done.4.refs_1_ = bf16[64,4096]{1,0:T(8,128)(2,1)S(1)} collective-permute-done((bf16[64,4096]{1,0:T(8,128)(2,1)S(1)}, bf16[64,4096]{1,0:T(8,128)(2,1)S(1)}, u32[]{:S(2)}, u32[]{:S(2)}) %collective-permute-start.4) | collective-permute-done | bytes 524320 | tf_op jit(solution)/shard_map/ppermute | solution.py:142
  153.6 0.5 collective-permute-start.8
  154.1 0.0 collective-permute-done.7.refs_4_
  154.1 0.0 collective-permute-done.10.refs_7_
  154.2 0.0 collective-permute-done.9.refs_6_
  154.2 0.8 copy-done.7
  155.0 0.8 collective-permute-done.8.refs_5_
  155.8 0.0 copy-done
  155.8 12.8 %from_blocks.1 = bf16[256,8192]{1,0:T(8,128)(2,1)} custom-call(s32[2]{0:T(128)} %pad_add_fusion.at, bf16[64,4096]{1,0:T(8,128)(2,1)} %copy-done, bf16[64,4096]{1,0:T(8,128)(2,1)} %copy-done.4, bf16[64,4096]{1,0:T(8,128)(2,1)} %copy-done.3, bf16[64,4096]{1,0:T(8,128)(2,1)} %copy-done.2, bf16[64,4096]{1,0:T(8,128)(2,1)} %copy-done.5, ...), custom_call_target="tpu_custom_call" | custom-call | tf_op jit(solution)/shard_map/from_blocks/pallas_call | solution.py:95
  (16 shorter events, 0.1 us)
Async XLA Ops:
  2.4 7.2 %collective-permute-start = (bf16[256,4096]{1,0:T(8,128)(2,1)S(1)}, bf16[256,4096]{1,0:T(8,128)(2,1)}, u32[]{:S(2)}, u32[]{:S(2)}) collective-permute-start(bf16[256,4096]{1,0:T(8,128)(2,1)S(1)} %dynamic-slice_bitcast_fusion), channel_id=1, source_target_pairs={{0,2},{2,0},{1,3},{3,1},{4,6},{6,4},{5,7},{7,5},{8,10},{10,8},{9,1... | collective-permute-start | bytes 6291464 | tf_op jit(solution)/shard_map/ppermute | solution.py:118
  18.2 29.4 %copy-start.1 = (f32[64,4096]{1,0:T(8,128)S(1)}, f32[64,4096]{1,0:T(8,128)}, u32[]{:S(2)}) copy-start(f32[64,4096]{1,0:T(8,128)} %get-tuple-element.7) | copy-start | bytes 3145732
  20.9 82.1 %copy-start.8 = (f32[1,2,8192]{2,1,0:T(2,128)S(1)}, f32[1,2,8192]{2,1,0:T(2,128)}, u32[]{:S(2)}) copy-start(f32[1,2,8192]{2,1,0:T(2,128)} %param.6) | copy-start | bytes 196612
  20.9 82.1 %copy-start.9 = (f32[1,2,8192]{2,1,0:T(2,128)S(1)}, f32[1,2,8192]{2,1,0:T(2,128)}, u32[]{:S(2)}) copy-start(f32[1,2,8192]{2,1,0:T(2,128)} %param.7) | copy-start | bytes 196612
  22.2 13.2 %collective-permute-start.3 = (f16[64,4096]{1,0:T(8,128)(2,1)S(1)}, f16[64,4096]{1,0:T(8,128)(2,1)S(1)}, u32[]{:S(2)}, u32[]{:S(2)}) collective-permute-start(f16[64,4096]{1,0:T(8,128)(2,1)S(1)} %convert_element_type.38), channel_id=1, source_target_pairs={{0,12},{4,0},{8,4},{12,8},{1,13},{5,1},{9,5},{13,9},{2,14},{6,2},{... | collective-permute-start | bytes 1572872 | tf_op jit(solution)/shard_map/ppermute | solution.py:120
  23.3 15.1 %collective-permute-start.2 = (f16[64,4096]{1,0:T(8,128)(2,1)S(1)}, f16[64,4096]{1,0:T(8,128)(2,1)S(1)}, u32[]{:S(2)}, u32[]{:S(2)}) collective-permute-start(f16[64,4096]{1,0:T(8,128)(2,1)S(1)} %convert_element_type.36), channel_id=1, source_target_pairs={{0,4},{4,8},{8,12},{12,0},{1,5},{5,9},{9,13},{13,1},{2,6},{6,10},{... | collective-permute-start | bytes 1572872 | tf_op jit(solution)/shard_map/ppermute | solution.py:120
  23.8 23.9 %collective-permute-start.1 = (f16[64,4096]{1,0:T(8,128)(2,1)S(1)}, f16[64,4096]{1,0:T(8,128)(2,1)S(1)}, u32[]{:S(2)}, u32[]{:S(2)}) collective-permute-start(f16[64,4096]{1,0:T(8,128)(2,1)S(1)} %convert_element_type.34), channel_id=1, source_target_pairs={{0,8},{4,12},{8,0},{12,4},{1,9},{5,13},{9,1},{13,5},{2,10},{6,14},... | collective-permute-start | bytes 1572872 | tf_op jit(solution)/shard_map/ppermute | solution.py:120
  126.5 29.3 %copy-start = (bf16[64,4096]{1,0:T(8,128)(2,1)}, bf16[64,4096]{1,0:T(8,128)(2,1)S(1)}, u32[]{:S(2)}) copy-start(bf16[64,4096]{1,0:T(8,128)(2,1)S(1)} %reshape.44.refs_0_) | copy-start | bytes 1572868
  126.5 11.5 %collective-permute-start.6 = (bf16[64,4096]{1,0:T(8,128)(2,1)S(1)}, bf16[64,4096]{1,0:T(8,128)(2,1)S(1)}, u32[]{:S(2)}, u32[]{:S(2)}) collective-permute-start(bf16[64,4096]{1,0:T(8,128)(2,1)S(1)} %reshape.44.refs_0_), channel_id=1, source_target_pairs={{0,12},{4,0},{8,4},{12,8},{1,13},{5,1},{9,5},{13,9},{2,14},{6,2},{... | collective-permute-start | bytes 1572872 | tf_op jit(solution)/shard_map/ppermute | solution.py:142
  127.1 16.4 %collective-permute-start.5 = (bf16[64,4096]{1,0:T(8,128)(2,1)S(1)}, bf16[64,4096]{1,0:T(8,128)(2,1)S(1)}, u32[]{:S(2)}, u32[]{:S(2)}) collective-permute-start(bf16[64,4096]{1,0:T(8,128)(2,1)S(1)} %reshape.44.refs_0_), channel_id=1, source_target_pairs={{0,8},{4,12},{8,0},{12,4},{1,9},{5,13},{9,1},{13,5},{2,10},{6,14},... | collective-permute-start | bytes 1572872 | tf_op jit(solution)/shard_map/ppermute | solution.py:142
  128.7 25.0 %collective-permute-start.4 = (bf16[64,4096]{1,0:T(8,128)(2,1)S(1)}, bf16[64,4096]{1,0:T(8,128)(2,1)S(1)}, u32[]{:S(2)}, u32[]{:S(2)}) collective-permute-start(bf16[64,4096]{1,0:T(8,128)(2,1)S(1)} %reshape.44.refs_0_), channel_id=1, source_target_pairs={{0,4},{4,8},{8,12},{12,0},{1,5},{5,9},{9,13},{13,1},{2,6},{6,10},{... | collective-permute-start | bytes 1572872 | tf_op jit(solution)/shard_map/ppermute | solution.py:142
  128.7 25.5 %collective-permute-start.7 = (bf16[64,4096]{1,0:T(8,128)(2,1)S(1)}, bf16[64,4096]{1,0:T(8,128)(2,1)S(1)}, u32[]{:S(2)}, u32[]{:S(2)}) collective-permute-start(bf16[64,4096]{1,0:T(8,128)(2,1)S(1)} %reshape.44.refs_0_), channel_id=1, source_target_pairs={{0,2},{2,0},{1,3},{3,1},{4,6},{6,4},{5,7},{7,5},{8,10},{10,8},{9,1... | collective-permute-start | bytes 1572872 | tf_op jit(solution)/shard_map/ppermute | solution.py:145
  138.0 17.8 %copy-start.2 = (bf16[64,4096]{1,0:T(8,128)(2,1)}, bf16[64,4096]{1,0:T(8,128)(2,1)S(1)}, u32[]{:S(2)}) copy-start(bf16[64,4096]{1,0:T(8,128)(2,1)S(1)} %collective-permute-done.6.refs_3_) | copy-start | bytes 1572868
  138.0 16.2 %collective-permute-start.10 = (bf16[64,4096]{1,0:T(8,128)(2,1)S(1)}, bf16[64,4096]{1,0:T(8,128)(2,1)S(1)}, u32[]{:S(2)}, u32[]{:S(2)}) collective-permute-start(bf16[64,4096]{1,0:T(8,128)(2,1)S(1)} %collective-permute-done.6.refs_3_), channel_id=1, source_target_pairs={{0,2},{2,0},{1,3},{3,1},{4,6},{6,4},{5,7},{7,5},{8,10},{10,8},{9,1... | collective-permute-start | bytes 1572872 | tf_op jit(solution)/shard_map/ppermute | solution.py:145
  143.4 12.4 %copy-start.3 = (bf16[64,4096]{1,0:T(8,128)(2,1)}, bf16[64,4096]{1,0:T(8,128)(2,1)S(1)}, u32[]{:S(2)}) copy-start(bf16[64,4096]{1,0:T(8,128)(2,1)S(1)} %collective-permute-done.5.refs_2_) | copy-start | bytes 1572868
  143.4 10.7 %collective-permute-start.9 = (bf16[64,4096]{1,0:T(8,128)(2,1)S(1)}, bf16[64,4096]{1,0:T(8,128)(2,1)S(1)}, u32[]{:S(2)}, u32[]{:S(2)}) collective-permute-start(bf16[64,4096]{1,0:T(8,128)(2,1)S(1)} %collective-permute-done.5.refs_2_), channel_id=1, source_target_pairs={{0,2},{2,0},{1,3},{3,1},{4,6},{6,4},{5,7},{7,5},{8,10},{10,8},{9,1... | collective-permute-start | bytes 1572872 | tf_op jit(solution)/shard_map/ppermute | solution.py:145
  153.6 2.2 %copy-start.4 = (bf16[64,4096]{1,0:T(8,128)(2,1)}, bf16[64,4096]{1,0:T(8,128)(2,1)S(1)}, u32[]{:S(2)}) copy-start(bf16[64,4096]{1,0:T(8,128)(2,1)S(1)} %collective-permute-done.4.refs_1_) | copy-start | bytes 1572868
  153.6 2.2 %collective-permute-start.8 = (bf16[64,4096]{1,0:T(8,128)(2,1)S(1)}, bf16[64,4096]{1,0:T(8,128)(2,1)}, u32[]{:S(2)}, u32[]{:S(2)}) collective-permute-start(bf16[64,4096]{1,0:T(8,128)(2,1)S(1)} %collective-permute-done.4.refs_1_), channel_id=1, source_target_pairs={{0,2},{2,0},{1,3},{3,1},{4,6},{6,4},{5,7},{7,5},{8,10},{10,8},{9,1... | collective-permute-start | bytes 1572872 | tf_op jit(solution)/shard_map/ppermute | solution.py:145
  154.1 1.7 copy-start.5
  154.2 1.7 copy-start.6
  154.2 0.9 copy-start.7
